TPU v7x, 512 devices: a whole 4x8x8 slice. The times are simulated.
512 devices in a mesh: sub: 128 (over z, y, core), grp: 4 (over x).
Axes of the slice: x: 4, y: 8, z: 8, core: 2. Of those that a mesh axis runs over, the one named last changes fastest.
Arguments:
- schur: bfloat16 [128, 2048, 2048], P('sub', 'grp'), may hold values from -0.125 to 0.125
- rhs: float32 [128, 2048, 192], P('sub', 'grp'), may hold values from -6 to 6
- start: float32 [128, 2048, 192], P('sub', 'grp'), may hold values from -6 to 6
- project: bfloat16 [128, 32, 4096], P('sub', 'grp'), may hold values from -0.75 to 0.75
- coarse_basis: bfloat16 [128, 8, 2048], P('sub', None, 'grp'), may hold values from -0.375 to 0.375
- owner_of_face: int32 [128, 32, 1], replicated, may hold values from 0 to 4; in each aligned block of 32 rows (0 to 31, 32 to 63, ..., all dimensions but the last counted through in order) at most 8 rows name the same one
- mortar_of_face: int32 [128, 32], replicated, may hold values from 0 to 15
- mortar_order: int32 [128, 16], replicated, may hold values from 3 to 7
- subdomain_map: int32 [128], replicated, may hold values from 0 to 127, each once
- vertex_ids: int32 [128, 8], replicated, may hold values from 0 to 255, all different within a row
Outputs:
- solution: float32 [128, 2048, 192], P('sub', 'grp')
Inputs may be any that keep to these rules, and one draw needn't show every extreme that they name: `owner_of_face`: the 32 faces of one subdomain name one offset at most 8 times. `mortar_of_face`: faces with the same owner and the same number lie on one mortar. `mortar_order`: row o holds the orders of the mortars owned by index o. `subdomain_map`: each subdomain once. `vertex_ids`: the 8 vertices of a subdomain differ; every vertex belongs to some subdomain.
All inputs are finite; a program needn't handle non-finite values.
Results may differ from a plain program's by a relative error of at most 0.0031.
Values may be sent and summed in bfloat16 or wider, within the bound.
A program may use at most 64 MiB of HBM per device.

v0:
```python
import jax
import jax.numpy as jnp
from jax import lax
from jax.sharding import Mesh
from jax.sharding import PartitionSpec as P

DEG = 8
FPTS = 64
MODES = 64
MORT_OWN = 16
ITERS = 2
REACH = 2
CAP = 8
SUB = ("sub_0", "sub_1", "sub_2")
relax_weight = 0.5
coarse_weight = 0.5


def joined_along(parts, dim):
    parts = jnp.moveaxis(parts, 0, dim)
    lengths = parts.shape
    return parts.reshape(*lengths[:dim], lengths[dim] * lengths[dim + 1], *lengths[dim + 2 :])


def sent_to_all(value, axis):
    copies = jnp.broadcast_to(value, (lax.axis_size(axis), *value.shape))
    return lax.all_to_all(copies, axis, split_axis=0, concat_axis=0, tiled=True)


def gathered_copies(value, axis, dim):
    return joined_along(sent_to_all(value, axis), dim)


def passed_along(value, axis, steps):
    count = lax.axis_size(axis)
    pairs = [(source, (source + steps) % count) for source in range(count)]
    return lax.ppermute(value, axis, pairs)


def taken_together(value, axis):
    return sent_to_all(value, axis).sum(axis=0)


def filled_up(lines, length):
    spare = -len(lines) % length
    return jnp.pad(lines, [(0, spare)] + [(0, 0)] * (lines.ndim - 1))


def whole_of(value, axes, dim):
    far, near = axes
    parts = sent_to_all(sent_to_all(value, far), near)
    return joined_along(parts.swapaxes(0, 1).reshape(-1, *value.shape), dim)


def split_up(value, dim, length):
    before, after = (value.shape[:dim], value.shape[dim + 1 :])
    return jnp.moveaxis(value.reshape(*before, length, -1, *after), dim, 0)


def sent_and_summed(value, axis, dim):
    parts = split_up(value, dim, lax.axis_size(axis))
    arrived = lax.all_to_all(parts, axis, split_axis=0, concat_axis=0, tiled=True)
    return arrived.sum(axis=0)


def summed_rows(value, axes, dim):
    far, near = axes
    parts = split_up(value, dim, lax.axis_size(far))
    nearer = sent_and_summed(parts, near, dim + 1)
    arrived = lax.all_to_all(nearer, far, split_axis=0, concat_axis=0, tiled=True)
    return arrived.sum(axis=0)


def sum_by_parts(value, axes):
    lines = value.reshape(-1, value.shape[-1])
    padded = filled_up(lines, lax.axis_size(axes[0]) * lax.axis_size(axes[1]))
    whole = whole_of(summed_rows(padded, axes, 0), axes, 0)
    return lax.slice_in_dim(whole, 0, len(lines)).reshape(value.shape)


def body(
    schur,
    rhs,
    start,
    project,
    coarse_basis,
    owner_of_face,
    mortar_of_face,
    mortar_order,
    subdomain_map,
    vertex_ids,
):
    highest = lax.Precision.HIGHEST
    contract_first = (((0,), (0,)), ((), ()))
    sub_count = lax.axis_size(SUB)
    position = lax.axis_index(SUB)
    all_faces = owner_of_face.shape[1]
    own_faces = project.shape[1]
    own_rows = schur.shape[1]
    neighbours = 2 * REACH + 1
    capacity = CAP
    vertices = 2 * sub_count
    held = jnp.take(owner_of_face[:, :, 0], subdomain_map, axis=0)
    mortar_local = jnp.take(mortar_of_face, subdomain_map, axis=0)
    face_index = jnp.arange(all_faces, dtype=jnp.int32)
    earlier = face_index[None, :] < face_index[:, None]
    ranks = jnp.sum(
        ((held[:, :, None] == held[:, None, :]) & earlier[None, :, :]).astype(jnp.int32), axis=2
    )
    my_held = lax.dynamic_index_in_dim(held, position, 0, keepdims=False)
    my_ranks = lax.dynamic_index_in_dim(ranks, position, 0, keepdims=False)
    slot_ids = my_held * capacity + my_ranks
    send_table = (
        jnp.arange(neighbours * capacity, dtype=jnp.int32)[:, None] == slot_ids[None, :]
    ).astype(jnp.bfloat16)
    links = jnp.arange(neighbours, dtype=jnp.int32)
    senders = jnp.mod(position - links + REACH, sub_count)
    from_held = jnp.take(held, senders, axis=0)
    from_mortar = jnp.take(mortar_local, senders, axis=0)
    from_ranks = jnp.take(ranks, senders, axis=0)
    incoming = (from_held == links[:, None]).astype(jnp.float32)
    mortar_hot = (
        from_mortar[:, :, None] == jnp.arange(MORT_OWN, dtype=jnp.int32)[None, None, :]
    ).astype(jnp.float32)
    rank_hot = (
        from_ranks[:, :, None] == jnp.arange(capacity, dtype=jnp.int32)[None, None, :]
    ).astype(jnp.float32)
    counts = jnp.einsum("jfk,jf->k", mortar_hot, incoming)
    degree = jnp.arange(MODES, dtype=jnp.int32)
    orders = lax.dynamic_index_in_dim(mortar_order, position, 0, keepdims=False)[:, None]
    keep_mask = ((degree[None, :] // DEG <= orders) & (degree[None, :] % DEG <= orders)).astype(
        jnp.float32
    )
    divisor = jnp.maximum(counts, 1.0)
    joined = jnp.einsum("jfk,jfc->kjc", mortar_hot * incoming[:, :, None], rank_hot)
    owner_table = joined.reshape(MORT_OWN, neighbours * capacity).astype(jnp.bfloat16)
    my_corners = lax.dynamic_index_in_dim(
        jnp.take(vertex_ids, subdomain_map, axis=0), position, 0, keepdims=False
    )
    corner_hot = (my_corners[:, None] == jnp.arange(vertices, dtype=jnp.int32)[None, :]).astype(
        jnp.float32
    )
    coarse_wide = coarse_basis[0].astype(jnp.float32)
    tables = project[0].reshape(own_faces, MODES, FPTS)
    matrix = schur[0]
    target = rhs[0]
    traces = start[0]
    for repeat in range(ITERS):
        trace_b = traces.astype(jnp.bfloat16)
        product = jnp.dot(
            matrix, gathered_copies(trace_b, "grp", 0), preferred_element_type=jnp.float32
        )
        residual = (product - target).astype(jnp.bfloat16)
        face_res = residual.reshape(own_faces, FPTS, -1)
        coeffs = jnp.einsum(
            "fmp,fpr->fmr", tables, face_res, preferred_element_type=jnp.float32
        ).astype(jnp.bfloat16)
        grouped = lax.all_to_all(coeffs, "grp", split_axis=2, concat_axis=0, tiled=True)
        part_rhs = grouped.shape[2]
        payload = grouped.reshape(all_faces, MODES * part_rhs)
        outgoing = jnp.dot(send_table, payload, preferred_element_type=jnp.float32).astype(
            jnp.bfloat16
        )
        blocks = outgoing.reshape(neighbours, capacity, -1)
        arrivals = []
        for link in range(neighbours):
            arrivals.append(passed_along(blocks[link], SUB, link - REACH))
        arrived = jnp.concatenate(arrivals, axis=0)
        mortar_sums = jnp.dot(owner_table, arrived, preferred_element_type=jnp.float32)
        shaped = mortar_sums.reshape(MORT_OWN, MODES, part_rhs) / divisor[:, None, None]
        shaped = shaped * keep_mask[:, :, None]
        averages = shaped.reshape(MORT_OWN, MODES * part_rhs).astype(jnp.bfloat16)
        replies = lax.dot_general(
            owner_table, averages, contract_first, preferred_element_type=jnp.float32
        ).astype(jnp.bfloat16)
        reply_blocks = replies.reshape(neighbours, capacity, -1)
        answers = []
        for link in range(neighbours):
            answers.append(passed_along(reply_blocks[link], SUB, REACH - link))
        answered = jnp.concatenate(answers, axis=0)
        own_back = lax.dot_general(
            send_table, answered, contract_first, preferred_element_type=jnp.float32
        ).astype(jnp.bfloat16)
        returned = lax.all_to_all(
            own_back.reshape(all_faces, MODES, part_rhs),
            "grp",
            split_axis=0,
            concat_axis=2,
            tiled=True,
        )
        lifted = jnp.einsum(
            "fmp,fmr->fpr", tables, returned, preferred_element_type=jnp.float32
        ).reshape(own_rows, -1)
        partial_value = jnp.dot(coarse_wide, lifted, precision=highest)
        summed = taken_together(partial_value, "grp")
        spread = lax.dot_general(corner_hot, summed, contract_first, precision=highest)
        vertex = sum_by_parts(spread, (("sub_0", "sub_1"), "sub_2"))
        picked = jnp.dot(corner_hot, vertex, precision=highest)
        coarse_corr = lax.dot_general(coarse_wide, picked, contract_first, precision=highest)
        traces = traces - relax_weight * lifted - coarse_weight * coarse_corr
    return traces[None]


def solution(mesh):
    finer = Mesh(
        mesh.devices.reshape(8, 8, 2, mesh.shape["grp"]), ("sub_0", "sub_1", "sub_2", "grp")
    )
    placed = (
        P(SUB, "grp", None),
        P(SUB, "grp", None),
        P(SUB, "grp", None),
        P(SUB, "grp", None),
        P(SUB, None, "grp"),
        P(),
        P(),
        P(),
        P(),
        P(),
    )
    return jax.shard_map(
        body, mesh=finer, in_specs=placed, out_specs=P(SUB, "grp", None), check_vma=False
    )
```

profile of v0, /device:TPU:1, one launch (start us, length us, event | category | flops | bytes accessed | tf_op | source)
XLA Modules:
  0.0 286.5 jit_solution(6291105881597627095)
XLA Ops:
  0.0 1.2 bitcast_convert_fusion
  2.2 5.0 %all-to-all-start = ((bf16[4,512,192]{1,2,0:T(8,128)(2,1)}), bf16[4,512,192]{1,2,0:T(8,128)(2,1)S(1)}, u32[]{:S(2)}, u32[]{:S(2)}) async-start(bf16[4,512,192]{1,2,0:T(8,128)(2,1)} %broadcast_in_dim.48), calls=%async_computation | async-start | bytes 1572864 | tf_op jit(solution)/shard_map/all_to_all | solution.py:27
  9.8 1.4 broadcast_select_fusion
  11.8 1.3 fusion.68
  13.3 1.4 gather_fusion.4
  15.4 1.0 reshape_squeeze.3
  20.9 1.0 reshape.341
  21.9 4.2 %all-to-all-start.1 = ((bf16[4,2,12288]{2,1,0:T(2,128)(2,1)}), bf16[4,2,12288]{2,1,0:T(2,128)(2,1)S(1)}, u32[]{:S(2)}, u32[]{:S(2)}) async-start(bf16[4,2,12288]{2,1,0:T(2,128)(2,1)} %reshape.341), calls=%async_computation.1 | async-start | bytes 393216 | tf_op jit(solution)/shard_map/all_to_all | solution.py:158
  26.2 5.1 %all-to-all-done.1 = bf16[4,2,12288]{2,1,0:T(2,128)(2,1)S(1)} async-done(((bf16[4,2,12288]{2,1,0:T(2,128)(2,1)}), bf16[4,2,12288]{2,1,0:T(2,128)(2,1)S(1)}, u32[]{:S(2)}, u32[]{:S(2)}) %all-to-all-start.1) | async-done | bytes 196640 | tf_op jit(solution)/shard_map/all_to_all | solution.py:158
  33.0 13.6 %collective-permute-start = (bf16[8,3072]{1,0:T(8,128)(2,1)S(1)}, bf16[8,3072]{1,0:T(8,128)(2,1)S(1)}, u32[]{:S(2)}, u32[]{:S(2)}) collective-permute-start(bf16[8,3072]{1,0:T(8,128)(2,1)S(1)} %get-tuple-element.28), channel_id=1, source_target_pairs={{0,504},{4,508},{8,0},{12,4},{16,8},{20,12},{24,16},{28,20},{32,24... | collective-permute-start | bytes 147464 | tf_op jit(solution)/shard_map/ppermute | solution.py:37
  46.7 1.9 collective-permute-start.4
  48.6 1.9 collective-permute-start.3
  50.6 4.9 %collective-permute-start.1 = (bf16[8,3072]{1,0:T(8,128)(2,1)S(1)}, bf16[8,3072]{1,0:T(8,128)(2,1)S(1)}, u32[]{:S(2)}, u32[]{:S(2)}) collective-permute-start(bf16[8,3072]{1,0:T(8,128)(2,1)S(1)} %get-tuple-element.27), channel_id=1, source_target_pairs={{0,508},{4,0},{8,4},{12,8},{16,12},{20,16},{24,20},{28,24},{32,28}... | collective-permute-start | bytes 147464 | tf_op jit(solution)/shard_map/ppermute | solution.py:37
  58.5 1.9 collective-permute-start.5
  60.4 12.5 %collective-permute-start.9 = (bf16[8,3072]{1,0:T(8,128)(2,1)S(1)}, bf16[8,3072]{1,0:T(8,128)(2,1)S(1)}, u32[]{:S(2)}, u32[]{:S(2)}) collective-permute-start(bf16[8,3072]{1,0:T(8,128)(2,1)S(1)} %get-tuple-element.19), channel_id=1, source_target_pairs={{0,504},{4,508},{8,0},{12,4},{16,8},{20,12},{24,16},{28,20},{32,24... | collective-permute-start | bytes 147464 | tf_op jit(solution)/shard_map/ppermute | solution.py:37
  72.9 2.5 collective-permute-start.8
  75.5 3.0 %collective-permute-start.6 = (bf16[8,3072]{1,0:T(8,128)(2,1)S(1)}, bf16[8,3072]{1,0:T(8,128)(2,1)S(1)}, u32[]{:S(2)}, u32[]{:S(2)}) collective-permute-start(bf16[8,3072]{1,0:T(8,128)(2,1)S(1)} %get-tuple-element.22), channel_id=1, source_target_pairs={{0,4},{4,8},{8,12},{12,16},{16,20},{20,24},{24,28},{28,32},{32,36}... | collective-permute-start | bytes 147464 | tf_op jit(solution)/shard_map/ppermute | solution.py:37
  78.5 1.1 collective-permute-done.6
  81.8 3.4 %all-to-all-start.2 = ((bf16[4,2,12288]{2,1,0:T(2,128)(2,1)}), bf16[4,2,12288]{2,1,0:T(2,128)(2,1)S(1)}, u32[]{:S(2)}, u32[]{:S(2)}) async-start(bf16[4,2,12288]{2,1,0:T(2,128)(2,1)} %reshape.343), calls=%async_computation.2 | async-start | bytes 393216 | tf_op jit(solution)/shard_map/all_to_all | solution.py:184
  86.7 3.6 %all-to-all-done.2 = bf16[4,2,12288]{2,1,0:T(2,128)(2,1)S(1)} async-done(((bf16[4,2,12288]{2,1,0:T(2,128)(2,1)}), bf16[4,2,12288]{2,1,0:T(2,128)(2,1)S(1)}, u32[]{:S(2)}, u32[]{:S(2)}) %all-to-all-start.2) | async-done | bytes 196640 | tf_op jit(solution)/shard_map/all_to_all | solution.py:184
  92.0 3.3 %all-to-all-start.3 = ((f32[4,8,192]{2,1,0:T(8,128)}), f32[4,8,192]{2,1,0:T(8,128)S(1)}, u32[]{:S(2)}, u32[]{:S(2)}) async-start(f32[4,8,192]{2,1,0:T(8,128)} %broadcast_in_dim.83), calls=%async_computation.3 | async-start | bytes 65536 | tf_op jit(solution)/shard_map/all_to_all | solution.py:27
  95.9 3.6 %all-to-all-done.3 = f32[4,8,192]{2,1,0:T(8,128)S(1)} async-done(((f32[4,8,192]{2,1,0:T(8,128)}), f32[4,8,192]{2,1,0:T(8,128)S(1)}, u32[]{:S(2)}, u32[]{:S(2)}) %all-to-all-start.3) | async-done | bytes 24608 | tf_op jit(solution)/shard_map/all_to_all | solution.py:27
  99.9 11.6 %all_to_all.126 = f32[2,64,2,192]{3,1,2,0:T(8,128)S(1)} all-to-all(f32[2,64,2,192]{3,1,2,0:T(8,128)S(1)} %convolution_bitcast_fusion.1), channel_id=1, replica_groups=mesh['sub_0'=8,'sub_1'=8,'sub_2'=2,'grp'=4] {'sub_2'}, dimensions={0} | all-to-all | bytes 393216 | tf_op jit(solution)/shard_map/all_to_all | solution.py:62
  111.7 15.4 %all_to_all.127 = f32[64,2,192]{2,1,0:T(2,128)S(1)} all-to-all(f32[64,2,192]{2,1,0:T(2,128)S(1)} %copy.170), channel_id=1, replica_groups=mesh['sub_0'=8,'sub_1'=8,'sub_2'=2,'grp'=4] {'sub_0','sub_1'}, dimensions={0} | all-to-all | bytes 196608 | tf_op jit(solution)/shard_map/all_to_all | solution.py:70
  127.9 5.5 %all-to-all-start.6 = ((f32[64,2,192]{2,1,0:T(2,128)}), f32[64,2,192]{2,1,0:T(2,128)}, u32[]{:S(2)}, u32[]{:S(2)}) async-start(f32[64,2,192]{2,1,0:T(2,128)} %broadcast_in_dim.84), calls=%async_computation.6 | async-start | bytes 262144 | tf_op jit(solution)/shard_map/all_to_all | solution.py:27
  133.6 11.2 %all-to-all-done.6 = f32[64,2,192]{2,1,0:T(2,128)} async-done(((f32[64,2,192]{2,1,0:T(2,128)}), f32[64,2,192]{2,1,0:T(2,128)}, u32[]{:S(2)}, u32[]{:S(2)}) %all-to-all-start.6) | async-done | bytes 98336 | tf_op jit(solution)/shard_map/all_to_all | solution.py:27
  145.8 6.8 %all_to_all.128 = f32[2,64,2,192]{3,2,1,0:T(2,128)S(1)} all-to-all(f32[2,64,2,192]{3,2,1,0:T(2,128)S(1)} %broadcast_in_dim.85), channel_id=1, replica_groups=mesh['sub_0'=8,'sub_1'=8,'sub_2'=2,'grp'=4] {'sub_2'}, dimensions={0} | all-to-all | bytes 393216 | tf_op jit(solution)/shard_map/all_to_all | solution.py:27
  153.0 1.2 fusion.73
  154.2 14.6 %all_to_all.129 = bf16[4,512,192]{1,2,0:T(8,128)(2,1)S(1)} all-to-all(bf16[4,512,192]{1,2,0:T(8,128)(2,1)S(1)} %broadcast_in_dim.86), channel_id=1, replica_groups=mesh['sub_0'=8,'sub_1'=8,'sub_2'=2,'grp'=4] {'grp'}, dimensions={0} | all-to-all | bytes 1572864 | tf_op jit(solution)/shard_map/all_to_all | solution.py:27
  170.7 7.5 %all_to_all.130 = bf16[4,2,12288]{2,1,0:T(2,128)(2,1)S(1)} all-to-all(bf16[4,2,12288]{2,1,0:T(2,128)(2,1)S(1)} %reshape.345), channel_id=1, replica_groups=mesh['sub_0'=8,'sub_1'=8,'sub_2'=2,'grp'=4] {'grp'}, dimensions={0} | all-to-all | bytes 393216 | tf_op jit(solution)/shard_map/all_to_all | solution.py:158
  179.9 2.2 collective-permute-start.10
  182.1 3.1 %collective-permute-start.14 = (bf16[8,3072]{1,0:T(8,128)(2,1)S(1)}, bf16[8,3072]{1,0:T(8,128)(2,1)S(1)}, u32[]{:S(2)}, u32[]{:S(2)}) collective-permute-start(bf16[8,3072]{1,0:T(8,128)(2,1)S(1)} %get-tuple-element.14), channel_id=1, source_target_pairs={{0,8},{4,12},{8,16},{12,20},{16,24},{20,28},{24,32},{28,36},{32,40... | collective-permute-start | bytes 147464 | tf_op jit(solution)/shard_map/ppermute | solution.py:37
  185.2 5.1 %collective-permute-start.13 = (bf16[8,3072]{1,0:T(8,128)(2,1)S(1)}, bf16[8,3072]{1,0:T(8,128)(2,1)S(1)}, u32[]{:S(2)}, u32[]{:S(2)}) collective-permute-start(bf16[8,3072]{1,0:T(8,128)(2,1)S(1)} %get-tuple-element.15), channel_id=1, source_target_pairs={{0,4},{4,8},{8,12},{12,16},{16,20},{20,24},{24,28},{28,32},{32,36}... | collective-permute-start | bytes 147464 | tf_op jit(solution)/shard_map/ppermute | solution.py:37
  190.3 1.9 collective-permute-start.11
  192.3 3.8 %collective-permute-done.11 = bf16[8,3072]{1,0:T(8,128)(2,1)S(1)} collective-permute-done((bf16[8,3072]{1,0:T(8,128)(2,1)S(1)}, bf16[8,3072]{1,0:T(8,128)(2,1)S(1)}, u32[]{:S(2)}, u32[]{:S(2)}) %collective-permute-start.11) | collective-permute-done | bytes 49184 | tf_op jit(solution)/shard_map/ppermute | solution.py:37
  198.9 2.0 collective-permute-start.15
  200.9 9.2 %collective-permute-start.19 = (bf16[8,3072]{1,0:T(8,128)(2,1)S(1)}, bf16[8,3072]{1,0:T(8,128)(2,1)S(1)}, u32[]{:S(2)}, u32[]{:S(2)}) collective-permute-start(bf16[8,3072]{1,0:T(8,128)(2,1)S(1)} %get-tuple-element.9), channel_id=1, source_target_pairs={{0,504},{4,508},{8,0},{12,4},{16,8},{20,12},{24,16},{28,20},{32,24... | collective-permute-start | bytes 147464 | tf_op jit(solution)/shard_map/ppermute | solution.py:37
  210.1 2.5 collective-permute-start.18
  212.7 3.0 %collective-permute-start.16 = (bf16[8,3072]{1,0:T(8,128)(2,1)S(1)}, bf16[8,3072]{1,0:T(8,128)(2,1)S(1)}, u32[]{:S(2)}, u32[]{:S(2)}) collective-permute-start(bf16[8,3072]{1,0:T(8,128)(2,1)S(1)} %get-tuple-element.12), channel_id=1, source_target_pairs={{0,4},{4,8},{8,12},{12,16},{16,20},{20,24},{24,28},{28,32},{32,36}... | collective-permute-start | bytes 147464 | tf_op jit(solution)/shard_map/ppermute | solution.py:37
  215.7 1.1 collective-permute-done.16
  218.3 7.5 %all_to_all.131 = bf16[4,2,12288]{2,1,0:T(2,128)(2,1)S(1)} all-to-all(bf16[4,2,12288]{2,1,0:T(2,128)(2,1)S(1)} %reshape.347), channel_id=1, replica_groups=mesh['sub_0'=8,'sub_1'=8,'sub_2'=2,'grp'=4] {'grp'}, dimensions={0} | all-to-all | bytes 393216 | tf_op jit(solution)/shard_map/all_to_all | solution.py:184
  226.9 6.7 %all_to_all.132 = f32[4,8,192]{2,1,0:T(8,128)S(1)} all-to-all(f32[4,8,192]{2,1,0:T(8,128)S(1)} %broadcast_in_dim.87), channel_id=1, replica_groups=mesh['sub_0'=8,'sub_1'=8,'sub_2'=2,'grp'=4] {'grp'}, dimensions={0} | all-to-all | bytes 49152 | tf_op jit(solution)/shard_map/all_to_all | solution.py:27
  233.9 11.6 %all_to_all.133 = f32[2,64,2,192]{3,1,2,0:T(8,128)S(1)} all-to-all(f32[2,64,2,192]{3,1,2,0:T(8,128)S(1)} %convolution_bitcast_fusion), channel_id=1, replica_groups=mesh['sub_0'=8,'sub_1'=8,'sub_2'=2,'grp'=4] {'sub_2'}, dimensions={0} | all-to-all | bytes 393216 | tf_op jit(solution)/shard_map/all_to_all | solution.py:62
  245.7 15.4 %all_to_all.134 = f32[64,2,192]{2,1,0:T(2,128)S(1)} all-to-all(f32[64,2,192]{2,1,0:T(2,128)S(1)} %copy.185), channel_id=1, replica_groups=mesh['sub_0'=8,'sub_1'=8,'sub_2'=2,'grp'=4] {'sub_0','sub_1'}, dimensions={0} | all-to-all | bytes 196608 | tf_op jit(solution)/shard_map/all_to_all | solution.py:70
  261.9 4.6 %all-to-all-start.14 = ((f32[64,2,192]{2,1,0:T(2,128)}), f32[64,2,192]{2,1,0:T(2,128)S(1)}, u32[]{:S(2)}, u32[]{:S(2)}) async-start(f32[64,2,192]{2,1,0:T(2,128)} %broadcast_in_dim.88), calls=%async_computation.14 | async-start | bytes 262144 | tf_op jit(solution)/shard_map/all_to_all | solution.py:27
  266.7 11.4 %all-to-all-done.14 = f32[64,2,192]{2,1,0:T(2,128)S(1)} async-done(((f32[64,2,192]{2,1,0:T(2,128)}), f32[64,2,192]{2,1,0:T(2,128)S(1)}, u32[]{:S(2)}, u32[]{:S(2)}) %all-to-all-start.14) | async-done | bytes 98336 | tf_op jit(solution)/shard_map/all_to_all | solution.py:27
  278.2 6.7 %all_to_all.135 = f32[2,64,2,192]{3,2,1,0:T(2,128)S(1)} all-to-all(f32[2,64,2,192]{3,2,1,0:T(2,128)S(1)} %broadcast_in_dim.89), channel_id=1, replica_groups=mesh['sub_0'=8,'sub_1'=8,'sub_2'=2,'grp'=4] {'sub_2'}, dimensions={0} | all-to-all | bytes 393216 | tf_op jit(solution)/shard_map/all_to_all | solution.py:27
  285.3 1.2 fusion.6
  (194 shorter events, 33.6 us)
Async XLA Ops:
  0.0 19.4 %copy-start = (bf16[1,512,2048]{2,1,0:T(8,128)(2,1)S(1)}, bf16[1,512,2048]{2,1,0:T(8,128)(2,1)}, u32[]{:S(2)}) copy-start(bf16[1,512,2048]{2,1,0:T(8,128)(2,1)} %param.14) | copy-start | bytes 6291460
  0.0 7.7 %copy-start.22 = (s32[128]{0:T(128)S(1)}, s32[128]{0:T(128)}, u32[]{:S(2)}) copy-start(s32[128]{0:T(128)} %param.22) | copy-start | bytes 1540
  0.0 8.2 %copy-start.8 = (s32[128,32,1]{0,2,1:T(1,128)S(1)}, s32[128,32,1]{0,2,1:T(1,128)}, u32[]{:S(2)}) copy-start(s32[128,32,1]{0,2,1:T(1,128)} %param.19) | copy-start | bytes 49156
  0.0 8.3 %copy-start.9 = (s32[128,32]{0,1:T(8,128)S(1)}, s32[128,32]{0,1:T(8,128)}, u32[]{:S(2)}) copy-start(s32[128,32]{0,1:T(8,128)} %param.20) | copy-start | bytes 49156
  2.2 14.3 %copy-start.12 = (s32[128,16]{0,1:T(8,128)S(1)}, s32[128,16]{0,1:T(8,128)}, u32[]{:S(2)}) copy-start(s32[128,16]{0,1:T(8,128)} %param.21) | copy-start | bytes 24580
  2.2 17.1 %all-to-all-start = ((bf16[4,512,192]{1,2,0:T(8,128)(2,1)}), bf16[4,512,192]{1,2,0:T(8,128)(2,1)S(1)}, u32[]{:S(2)}, u32[]{:S(2)}) async-start(bf16[4,512,192]{1,2,0:T(8,128)(2,1)} %broadcast_in_dim.48), calls=%async_computation | async-start | bytes 1572864 | tf_op jit(solution)/shard_map/all_to_all | solution.py:27
  7.1 12.3 %copy-start.3 = (f32[1,512,192]{1,2,0:T(8,128)S(1)}, f32[1,512,192]{1,2,0:T(8,128)}, u32[]{:S(2)}) copy-start(f32[1,512,192]{1,2,0:T(8,128)} %param.15) | copy-start | bytes 1179652
  8.5 6.2 %copy-start.14 = (s32[1024]{0:T(1024)}, s32[1024]{0:T(1024)S(1)}, u32[]{:S(2)}) copy-start(s32[1024]{0:T(1024)S(1)} %get-tuple-element.37) | copy-start | bytes 12292
  19.3 38.9 %copy-start.6 = (bf16[5,8,16]{2,1,0:T(8,128)(2,1)}, bf16[5,8,16]{2,1,0:T(8,128)(2,1)S(1)}, u32[]{:S(2)}) copy-start(bf16[5,8,16]{2,1,0:T(8,128)(2,1)S(1)} %convolution_convert_fusion.8) | copy-start | bytes 3844
  20.3 5.9 %copy-start.17 = (s32[16]{0:T(128)S(1)}, s32[16]{0:T(128)}, u32[]{:S(2)}) copy-start(s32[16]{0:T(128)} %dynamic-slice_reduce_fusion) | copy-start | bytes 196
  20.3 5.9 %copy-start.20 = (s32[64]{0:T(128)S(1)}, s32[64]{0:T(128)}, u32[]{:S(2)}) copy-start(s32[64]{0:T(128)} %get-tuple-element.35) | copy-start | bytes 772
  20.9 25.7 %copy-start.18 = (pred[5,32]{1,0:T(8,128)(4,1)S(1)}, pred[5,32]{1,0:T(8,128)(4,1)}, u32[]{:S(2)}) copy-start(pred[5,32]{1,0:T(8,128)(4,1)} %get-tuple-element.8) | copy-start | bytes 484
  21.9 9.4 %all-to-all-start.1 = ((bf16[4,2,12288]{2,1,0:T(2,128)(2,1)}), bf16[4,2,12288]{2,1,0:T(2,128)(2,1)S(1)}, u32[]{:S(2)}, u32[]{:S(2)}) async-start(bf16[4,2,12288]{2,1,0:T(2,128)(2,1)} %reshape.341), calls=%async_computation.1 | async-start | bytes 393216 | tf_op jit(solution)/shard_map/all_to_all | solution.py:158
  26.2 55.6 %copy-start.13 = (f32[16,64]{1,0:T(8,128)}, f32[16,64]{1,0:T(8,128)S(1)}, u32[]{:S(2)}) copy-start(f32[16,64]{1,0:T(8,128)S(1)} %and_convert_fusion) | copy-start | bytes 12292
  26.2 53.5 %copy-start.10 = (s32[32]{0:T(128)}, s32[32]{0:T(128)S(1)}, u32[]{:S(2)}) copy-start(s32[32]{0:T(128)S(1)} %fusion.66) | copy-start | bytes 388
  33.0 22.4 %collective-permute-start = (bf16[8,3072]{1,0:T(8,128)(2,1)S(1)}, bf16[8,3072]{1,0:T(8,128)(2,1)S(1)}, u32[]{:S(2)}, u32[]{:S(2)}) collective-permute-start(bf16[8,3072]{1,0:T(8,128)(2,1)S(1)} %get-tuple-element.28), channel_id=1, source_target_pairs={{0,504},{4,508},{8,0},{12,4},{16,8},{20,12},{24,16},{28,20},{32,24... | collective-permute-start | bytes 147464 | tf_op jit(solution)/shard_map/ppermute | solution.py:37
  46.7 11.2 %copy-start.23 = (f32[16]{0:T(128)}, f32[16]{0:T(128)S(1)}, u32[]{:S(2)}) copy-start(f32[16]{0:T(128)S(1)} %fusion.30) | copy-start | bytes 196
  46.7 9.6 %collective-permute-start.4 = (bf16[8,3072]{1,0:T(8,128)(2,1)S(1)}, bf16[8,3072]{1,0:T(8,128)(2,1)S(1)}, u32[]{:S(2)}, u32[]{:S(2)}) collective-permute-start(bf16[8,3072]{1,0:T(8,128)(2,1)S(1)} %get-tuple-element.24), channel_id=1, source_target_pairs={{0,8},{4,12},{8,16},{12,20},{16,24},{20,28},{24,32},{28,36},{32,40... | collective-permute-start | bytes 147464 | tf_op jit(solution)/shard_map/ppermute | solution.py:37
  48.6 7.7 %collective-permute-start.3 = (bf16[8,3072]{1,0:T(8,128)(2,1)S(1)}, bf16[8,3072]{1,0:T(8,128)(2,1)S(1)}, u32[]{:S(2)}, u32[]{:S(2)}) collective-permute-start(bf16[8,3072]{1,0:T(8,128)(2,1)S(1)} %get-tuple-element.25), channel_id=1, source_target_pairs={{0,4},{4,8},{8,12},{12,16},{16,20},{20,24},{24,28},{28,32},{32,36}... | collective-permute-start | bytes 147464 | tf_op jit(solution)/shard_map/ppermute | solution.py:37
  50.5 5.7 %collective-permute-start.2 = (bf16[8,3072]{1,0:T(8,128)(2,1)S(1)}, bf16[8,3072]{1,0:T(8,128)(2,1)S(1)}, u32[]{:S(2)}, u32[]{:S(2)}) collective-permute-start(bf16[8,3072]{1,0:T(8,128)(2,1)S(1)} %get-tuple-element.26), channel_id=1, source_target_pairs={{0,0},{4,4},{8,8},{12,12},{16,16},{20,20},{24,24},{28,28},{32,32},... | collective-permute-start | bytes 147464 | tf_op jit(solution)/shard_map/ppermute | solution.py:37
  50.6 5.7 %collective-permute-start.1 = (bf16[8,3072]{1,0:T(8,128)(2,1)S(1)}, bf16[8,3072]{1,0:T(8,128)(2,1)S(1)}, u32[]{:S(2)}, u32[]{:S(2)}) collective-permute-start(bf16[8,3072]{1,0:T(8,128)(2,1)S(1)} %get-tuple-element.27), channel_id=1, source_target_pairs={{0,508},{4,0},{8,4},{12,8},{16,12},{20,16},{24,20},{28,24},{32,28}... | collective-permute-start | bytes 147464 | tf_op jit(solution)/shard_map/ppermute | solution.py:37
  58.4 26.8 %copy-start.19 = (pred[128]{0:T(512)(128)(4,1)S(1)}, pred[128]{0:T(512)(128)(4,1)}, u32[]{:S(2)}) copy-start(pred[128]{0:T(512)(128)(4,1)} %compare_and_fusion.1) | copy-start | bytes 388
  58.4 27.4 %copy-start.16 = (s32[128,8]{0,1:T(8,128)S(1)}, s32[128,8]{0,1:T(8,128)}, u32[]{:S(2)}) copy-start(s32[128,8]{0,1:T(8,128)} %param.23) | copy-start | bytes 12292
  58.5 20.1 %collective-permute-start.5 = (bf16[8,3072]{1,0:T(8,128)(2,1)S(1)}, bf16[8,3072]{1,0:T(8,128)(2,1)S(1)}, u32[]{:S(2)}, u32[]{:S(2)}) collective-permute-start(bf16[8,3072]{1,0:T(8,128)(2,1)S(1)} %get-tuple-element.23), channel_id=1, source_target_pairs={{0,8},{4,12},{8,16},{12,20},{16,24},{20,28},{24,32},{28,36},{32,40... | collective-permute-start | bytes 147464 | tf_op jit(solution)/shard_map/ppermute | solution.py:37
  60.4 19.3 %collective-permute-start.9 = (bf16[8,3072]{1,0:T(8,128)(2,1)S(1)}, bf16[8,3072]{1,0:T(8,128)(2,1)S(1)}, u32[]{:S(2)}, u32[]{:S(2)}) collective-permute-start(bf16[8,3072]{1,0:T(8,128)(2,1)S(1)} %get-tuple-element.19), channel_id=1, source_target_pairs={{0,504},{4,508},{8,0},{12,4},{16,8},{20,12},{24,16},{28,20},{32,24... | collective-permute-start | bytes 147464 | tf_op jit(solution)/shard_map/ppermute | solution.py:37
  72.9 6.8 %collective-permute-start.8 = (bf16[8,3072]{1,0:T(8,128)(2,1)S(1)}, bf16[8,3072]{1,0:T(8,128)(2,1)S(1)}, u32[]{:S(2)}, u32[]{:S(2)}) collective-permute-start(bf16[8,3072]{1,0:T(8,128)(2,1)S(1)} %get-tuple-element.20), channel_id=1, source_target_pairs={{0,508},{4,0},{8,4},{12,8},{16,12},{20,16},{24,20},{28,24},{32,28}... | collective-permute-start | bytes 147464 | tf_op jit(solution)/shard_map/ppermute | solution.py:37
  75.5 4.2 %collective-permute-start.7 = (bf16[8,3072]{1,0:T(8,128)(2,1)S(1)}, bf16[8,3072]{1,0:T(8,128)(2,1)S(1)}, u32[]{:S(2)}, u32[]{:S(2)}) collective-permute-start(bf16[8,3072]{1,0:T(8,128)(2,1)S(1)} %get-tuple-element.21), channel_id=1, source_target_pairs={{0,0},{4,4},{8,8},{12,12},{16,16},{20,20},{24,24},{28,28},{32,32},... | collective-permute-start | bytes 147464 | tf_op jit(solution)/shard_map/ppermute | solution.py:37
  75.5 4.2 %collective-permute-start.6 = (bf16[8,3072]{1,0:T(8,128)(2,1)S(1)}, bf16[8,3072]{1,0:T(8,128)(2,1)S(1)}, u32[]{:S(2)}, u32[]{:S(2)}) collective-permute-start(bf16[8,3072]{1,0:T(8,128)(2,1)S(1)} %get-tuple-element.22), channel_id=1, source_target_pairs={{0,4},{4,8},{8,12},{12,16},{16,20},{20,24},{24,28},{28,32},{32,36}... | collective-permute-start | bytes 147464 | tf_op jit(solution)/shard_map/ppermute | solution.py:37
  80.8 10.2 %copy-start.5 = (bf16[1,8,512]{2,1,0:T(8,128)(2,1)S(1)}, bf16[1,8,512]{2,1,0:T(8,128)(2,1)}, u32[]{:S(2)}) copy-start(bf16[1,8,512]{2,1,0:T(8,128)(2,1)} %param.18) | copy-start | bytes 24580
  81.8 8.5 %all-to-all-start.2 = ((bf16[4,2,12288]{2,1,0:T(2,128)(2,1)}), bf16[4,2,12288]{2,1,0:T(2,128)(2,1)S(1)}, u32[]{:S(2)}, u32[]{:S(2)}) async-start(bf16[4,2,12288]{2,1,0:T(2,128)(2,1)} %reshape.343), calls=%async_computation.2 | async-start | bytes 393216 | tf_op jit(solution)/shard_map/all_to_all | solution.py:184
  92.0 7.5 %all-to-all-start.3 = ((f32[4,8,192]{2,1,0:T(8,128)}), f32[4,8,192]{2,1,0:T(8,128)S(1)}, u32[]{:S(2)}, u32[]{:S(2)}) async-start(f32[4,8,192]{2,1,0:T(8,128)} %broadcast_in_dim.83), calls=%async_computation.3 | async-start | bytes 65536 | tf_op jit(solution)/shard_map/all_to_all | solution.py:27
  111.6 41.4 %copy-start.1 = (f32[1,512,192]{1,2,0:T(8,128)S(1)}, f32[1,512,192]{1,2,0:T(8,128)}, u32[]{:S(2)}) copy-start(f32[1,512,192]{1,2,0:T(8,128)} %param.16) | copy-start | bytes 1179652
  127.9 16.9 %all-to-all-start.6 = ((f32[64,2,192]{2,1,0:T(2,128)}), f32[64,2,192]{2,1,0:T(2,128)}, u32[]{:S(2)}, u32[]{:S(2)}) async-start(f32[64,2,192]{2,1,0:T(2,128)} %broadcast_in_dim.84), calls=%async_computation.6 | async-start | bytes 262144 | tf_op jit(solution)/shard_map/all_to_all | solution.py:27
  154.1 14.8 %copy-start.4 = (f32[1,512,192]{1,2,0:T(8,128)S(1)}, f32[1,512,192]{1,2,0:T(8,128)}, u32[]{:S(2)}) copy-start(f32[1,512,192]{1,2,0:T(8,128)} %param.15) | copy-start | bytes 1179652
  170.1 9.5 %copy-start.11 = (s32[32]{0:T(128)S(1)}, s32[32]{0:T(128)}, u32[]{:S(2)}) copy-start(s32[32]{0:T(128)} %copy-done.10) | copy-start | bytes 388
  178.9 18.2 %copy-start.7 = (bf16[5,8,16]{2,1,0:T(8,128)(2,1)S(1)}, bf16[5,8,16]{2,1,0:T(8,128)(2,1)}, u32[]{:S(2)}) copy-start(bf16[5,8,16]{2,1,0:T(8,128)(2,1)} %copy-done.6) | copy-start | bytes 3844
  179.9 12.3 %collective-permute-start.10 = (bf16[8,3072]{1,0:T(8,128)(2,1)S(1)}, bf16[8,3072]{1,0:T(8,128)(2,1)S(1)}, u32[]{:S(2)}, u32[]{:S(2)}) collective-permute-start(bf16[8,3072]{1,0:T(8,128)(2,1)S(1)} %get-tuple-element.18), channel_id=1, source_target_pairs={{0,504},{4,508},{8,0},{12,4},{16,8},{20,12},{24,16},{28,20},{32,24... | collective-permute-start | bytes 147464 | tf_op jit(solution)/shard_map/ppermute | solution.py:37
  182.1 14.0 %collective-permute-start.14 = (bf16[8,3072]{1,0:T(8,128)(2,1)S(1)}, bf16[8,3072]{1,0:T(8,128)(2,1)S(1)}, u32[]{:S(2)}, u32[]{:S(2)}) collective-permute-start(bf16[8,3072]{1,0:T(8,128)(2,1)S(1)} %get-tuple-element.14), channel_id=1, source_target_pairs={{0,8},{4,12},{8,16},{12,20},{16,24},{20,28},{24,32},{28,36},{32,40... | collective-permute-start | bytes 147464 | tf_op jit(solution)/shard_map/ppermute | solution.py:37
  185.2 10.8 %collective-permute-start.13 = (bf16[8,3072]{1,0:T(8,128)(2,1)S(1)}, bf16[8,3072]{1,0:T(8,128)(2,1)S(1)}, u32[]{:S(2)}, u32[]{:S(2)}) collective-permute-start(bf16[8,3072]{1,0:T(8,128)(2,1)S(1)} %get-tuple-element.15), channel_id=1, source_target_pairs={{0,4},{4,8},{8,12},{12,16},{16,20},{20,24},{24,28},{28,32},{32,36}... | collective-permute-start | bytes 147464 | tf_op jit(solution)/shard_map/ppermute | solution.py:37
  190.3 5.7 %collective-permute-start.12 = (bf16[8,3072]{1,0:T(8,128)(2,1)S(1)}, bf16[8,3072]{1,0:T(8,128)(2,1)S(1)}, u32[]{:S(2)}, u32[]{:S(2)}) collective-permute-start(bf16[8,3072]{1,0:T(8,128)(2,1)S(1)} %get-tuple-element.16), channel_id=1, source_target_pairs={{0,0},{4,4},{8,8},{12,12},{16,16},{20,20},{24,24},{28,28},{32,32},... | collective-permute-start | bytes 147464 | tf_op jit(solution)/shard_map/ppermute | solution.py:37
  190.3 5.7 %collective-permute-start.11 = (bf16[8,3072]{1,0:T(8,128)(2,1)S(1)}, bf16[8,3072]{1,0:T(8,128)(2,1)S(1)}, u32[]{:S(2)}, u32[]{:S(2)}) collective-permute-start(bf16[8,3072]{1,0:T(8,128)(2,1)S(1)} %get-tuple-element.17), channel_id=1, source_target_pairs={{0,508},{4,0},{8,4},{12,8},{16,12},{20,16},{24,20},{28,24},{32,28}... | collective-permute-start | bytes 147464 | tf_op jit(solution)/shard_map/ppermute | solution.py:37
  198.9 16.8 %collective-permute-start.15 = (bf16[8,3072]{1,0:T(8,128)(2,1)S(1)}, bf16[8,3072]{1,0:T(8,128)(2,1)S(1)}, u32[]{:S(2)}, u32[]{:S(2)}) collective-permute-start(bf16[8,3072]{1,0:T(8,128)(2,1)S(1)} %get-tuple-element.13), channel_id=1, source_target_pairs={{0,8},{4,12},{8,16},{12,20},{16,24},{20,28},{24,32},{28,36},{32,40... | collective-permute-start | bytes 147464 | tf_op jit(solution)/shard_map/ppermute | solution.py:37
  200.9 16.0 %collective-permute-start.19 = (bf16[8,3072]{1,0:T(8,128)(2,1)S(1)}, bf16[8,3072]{1,0:T(8,128)(2,1)S(1)}, u32[]{:S(2)}, u32[]{:S(2)}) collective-permute-start(bf16[8,3072]{1,0:T(8,128)(2,1)S(1)} %get-tuple-element.9), channel_id=1, source_target_pairs={{0,504},{4,508},{8,0},{12,4},{16,8},{20,12},{24,16},{28,20},{32,24... | collective-permute-start | bytes 147464 | tf_op jit(solution)/shard_map/ppermute | solution.py:37
  210.1 6.8 %collective-permute-start.18 = (bf16[8,3072]{1,0:T(8,128)(2,1)S(1)}, bf16[8,3072]{1,0:T(8,128)(2,1)S(1)}, u32[]{:S(2)}, u32[]{:S(2)}) collective-permute-start(bf16[8,3072]{1,0:T(8,128)(2,1)S(1)} %get-tuple-element.10), channel_id=1, source_target_pairs={{0,508},{4,0},{8,4},{12,8},{16,12},{20,16},{24,20},{28,24},{32,28}... | collective-permute-start | bytes 147464 | tf_op jit(solution)/shard_map/ppermute | solution.py:37
  212.7 4.2 %collective-permute-start.17 = (bf16[8,3072]{1,0:T(8,128)(2,1)S(1)}, bf16[8,3072]{1,0:T(8,128)(2,1)S(1)}, u32[]{:S(2)}, u32[]{:S(2)}) collective-permute-start(bf16[8,3072]{1,0:T(8,128)(2,1)S(1)} %get-tuple-element.11), channel_id=1, source_target_pairs={{0,0},{4,4},{8,8},{12,12},{16,16},{20,20},{24,24},{28,28},{32,32},... | collective-permute-start | bytes 147464 | tf_op jit(solution)/shard_map/ppermute | solution.py:37
  212.7 4.2 %collective-permute-start.16 = (bf16[8,3072]{1,0:T(8,128)(2,1)S(1)}, bf16[8,3072]{1,0:T(8,128)(2,1)S(1)}, u32[]{:S(2)}, u32[]{:S(2)}) collective-permute-start(bf16[8,3072]{1,0:T(8,128)(2,1)S(1)} %get-tuple-element.12), channel_id=1, source_target_pairs={{0,4},{4,8},{8,12},{12,16},{16,20},{20,24},{24,28},{28,32},{32,36}... | collective-permute-start | bytes 147464 | tf_op jit(solution)/shard_map/ppermute | solution.py:37
  245.6 39.7 %copy-start.2 = (f32[512,192]{0,1:T(8,128)S(1)}, f32[512,192]{0,1:T(8,128)}, u32[]{:S(2)}) copy-start(f32[512,192]{0,1:T(8,128)} %get-tuple-element.34) | copy-start | bytes 1179652
  261.9 16.2 %all-to-all-start.14 = ((f32[64,2,192]{2,1,0:T(2,128)}), f32[64,2,192]{2,1,0:T(2,128)S(1)}, u32[]{:S(2)}, u32[]{:S(2)}) async-start(f32[64,2,192]{2,1,0:T(2,128)} %broadcast_in_dim.88), calls=%async_computation.14 | async-start | bytes 262144 | tf_op jit(solution)/shard_map/all_to_all | solution.py:27
  (2 other events, 6.5 us)
where the time goes:
time: 288 us; the launch traced here: 286 us
  blocking collectives  104 us (36%)
  starting transfers between devices  97.3 us (34%)
  waiting for transfers between devices  41.8 us (15%)
  local copies, waits for them, and re-layouts  24.6 us (9%)
  matrix products  10.3 us (4%)
  other arithmetic  7.34 us (3%)
    ppermute x20, starting transfers between devices, passed_along(): return lax.ppermute(value, axis, pairs)  71.4 us
    all_to_all x4, blocking collectives, sent_to_all(): return lax.all_to_all(copies, axis, split_axis=0, concat_axis=0, tiled=True)  34.8 us
    all_to_all x2, blocking collectives, summed_rows(): lax.all_to_all(nearer, far, split_axis=0, concat_axis=0, tiled=True)  30.9 us
    all_to_all x4, waiting for transfers between devices, sent_to_all(): return lax.all_to_all(copies, axis, split_axis=0, concat_axis=0, tiled=True)  26.2 us
    all_to_all x2, blocking collectives, sent_and_summed(): lax.all_to_all(parts, axis, split_axis=0, concat_axis=0, tiled=True)  23.3 us
    all_to_all x4, starting transfers between devices, sent_to_all(): return lax.all_to_all(copies, axis, split_axis=0, concat_axis=0, tiled=True)  18.3 us
    all_to_all x1, blocking collectives, body(): lax.all_to_all(coeffs, 'grp', split_axis=2, concat_axis=0, tiled=True)  7.54 us
    all_to_all x1, blocking collectives, body(): lax.all_to_all(own_back.reshape(all_faces, MODES, part_rhs), 'grp', split...  7.54 us
  transfers between devices with their start and end apart: 26, of which 9 were waited for; matrix products, arithmetic and copies ran while one was open for 5% of the time, Pallas kernels for 0%

commit v1 on v0

--- a/solution.py
+++ b/solution.py
@@ -14,6 +14,18 @@
 SUB = ("sub_0", "sub_1", "sub_2")
 relax_weight = 0.5
 coarse_weight = 0.5
+
+
+def rotated_exchange(x, axis, split, join):
+    ways, here = (lax.axis_size(axis), lax.axis_index(axis))
+    width = x.shape[split] // ways
+    turned = jnp.roll(x, -here * width, axis=split)
+    got = [lax.slice_in_dim(turned, 0, width, axis=split)]
+    for far in range(1, ways):
+        sent = lax.slice_in_dim(turned, far * width, (far + 1) * width, axis=split)
+        got.append(lax.ppermute(sent, axis, [(d, (d + far) % ways) for d in range(ways)]))
+    line = jnp.concatenate(got[::-1], axis=join)
+    return jnp.roll(line, (here + 1) * got[0].shape[join], axis=join)
 
 
 def joined_along(parts, dim):
@@ -155,7 +167,7 @@
         coeffs = jnp.einsum(
             "fmp,fpr->fmr", tables, face_res, preferred_element_type=jnp.float32
         ).astype(jnp.bfloat16)
-        grouped = lax.all_to_all(coeffs, "grp", split_axis=2, concat_axis=0, tiled=True)
+        grouped = rotated_exchange(coeffs, "grp", 2, 0)
         part_rhs = grouped.shape[2]
         payload = grouped.reshape(all_faces, MODES * part_rhs)
         outgoing = jnp.dot(send_table, payload, preferred_element_type=jnp.float32).astype(

time: 288 us -> 301 us (1.045)
  starting transfers between devices: 97.3 us -> 112 us
  blocking collectives: 104 us -> 97.7 us
  other arithmetic: 7.34 us -> 10.8 us
    ppermute x0 -> x6, starting transfers between devices: none -> 19.2 us  [rotated_exchange(): lax.ppermute(sent, axis, [(d, (d + far) % ways) for d in range(ways)])]
    all_to_all x1 -> x0, blocking collectives: 7.54 us -> none  [body(): lax.all_to_all(coeffs, 'grp', split_axis=2, concat_axis=0, tiled=True)]
    ppermute x0 -> x6, waiting for transfers between devices: none -> 7.51 us  [rotated_exchange(): lax.ppermute(sent, axis, [(d, (d + far) % ways) for d in range(ways)])]
    all_to_all x1 -> x0, waiting for transfers between devices: 5.07 us -> none  [body(): lax.all_to_all(coeffs, 'grp', split_axis=2, concat_axis=0, tiled=True)]
    all_to_all x1 -> x0, starting transfers between devices: 4.24 us -> none  [body(): lax.all_to_all(coeffs, 'grp', split_axis=2, concat_axis=0, tiled=True)]
    concatenate x0 -> x4, other arithmetic: none -> 3.38 us  [the longest x2 2.79 us: rotated_exchange(): return jnp.roll(line, (here + 1) * got[0].shape[join], axis=join)]
  transfers between devices with their start and end apart: 26 -> 31, of which waited for: 9 -> 11; matrix products, arithmetic and copies ran while one was open for 5% -> 5% of each run, Pallas kernels for 0% -> 0%
where the time goes in v1:
time: 301 us; the launch traced here: 299 us
  starting transfers between devices  112 us (37%)
  blocking collectives  97.7 us (32%)
  waiting for transfers between devices  44.1 us (15%)
  local copies, waits for them, and re-layouts  22.6 us (8%)
  matrix products  10.9 us (4%)
  other arithmetic  10.8 us (4%)
    ppermute x20, starting transfers between devices, passed_along(): return lax.ppermute(value, axis, pairs)  70.9 us
    all_to_all x4, blocking collectives, sent_to_all(): return lax.all_to_all(copies, axis, split_axis=0, concat_axis=0, tiled=True)  34.7 us
    all_to_all x2, blocking collectives, summed_rows(): lax.all_to_all(nearer, far, split_axis=0, concat_axis=0, tiled=True)  30.9 us
    all_to_all x4, waiting for transfers between devices, sent_to_all(): return lax.all_to_all(copies, axis, split_axis=0, concat_axis=0, tiled=True)  26 us
    all_to_all x2, blocking collectives, sent_and_summed(): lax.all_to_all(parts, axis, split_axis=0, concat_axis=0, tiled=True)  23.9 us
    ppermute x6, starting transfers between devices, rotated_exchange(): lax.ppermute(sent, axis, [(d, (d + far) % ways) for d in range(ways)])  19.2 us
    all_to_all x4, starting transfers between devices, sent_to_all(): return lax.all_to_all(copies, axis, split_axis=0, concat_axis=0, tiled=True)  18.3 us
    all_to_all x1, blocking collectives, body(): lax.all_to_all(own_back.reshape(all_faces, MODES, part_rhs), 'grp', split...  8.32 us
  transfers between devices with their start and end apart: 31, of which 11 were waited for; matrix products, arithmetic and copies ran while one was open for 5% of the time, Pallas kernels for 0%

profile of v1, /device:TPU:1, one launch (start us, length us, event | category | flops | bytes accessed | tf_op | source)
XLA Modules:
  0.0 299.4 jit_solution(7571470210966388886)
XLA Ops:
  2.2 4.8 %all-to-all-start = ((bf16[4,512,192]{1,2,0:T(8,128)(2,1)}), bf16[4,512,192]{1,2,0:T(8,128)(2,1)S(1)}, u32[]{:S(2)}, u32[]{:S(2)}) async-start(bf16[4,512,192]{1,2,0:T(8,128)(2,1)} %broadcast_in_dim.48), calls=%async_computation | async-start | bytes 1572864 | tf_op jit(solution)/shard_map/all_to_all | solution.py:39
  11.0 1.4 gather_fusion.4
  15.2 1.3 and_convert_fusion
  16.5 1.3 fusion.84
  21.1 3.4 %collective-permute-start.2 = (bf16[8,64,48]{2,1,0:T(8,128)(2,1)S(1)}, bf16[8,64,48]{2,1,0:T(8,128)(2,1)S(1)}, u32[]{:S(2)}, u32[]{:S(2)}) collective-permute-start(bf16[8,64,48]{2,1,0:T(8,128)(2,1)S(1)} %get-tuple-element.16), channel_id=1, source_target_pairs={{0,1},{1,2},{2,3},{3,0},{4,5},{5,6},{6,7},{7,4},{8,9},{9,10},{10,1... | collective-permute-start | bytes 147464 | tf_op jit(solution)/shard_map/ppermute | solution.py:26
  24.4 4.3 %collective-permute-start.1 = (bf16[8,64,48]{2,1,0:T(8,128)(2,1)S(1)}, bf16[8,64,48]{2,1,0:T(8,128)(2,1)S(1)}, u32[]{:S(2)}, u32[]{:S(2)}) collective-permute-start(bf16[8,64,48]{2,1,0:T(8,128)(2,1)S(1)} %get-tuple-element.17), channel_id=1, source_target_pairs={{0,2},{1,3},{2,0},{3,1},{4,6},{5,7},{6,4},{7,5},{8,10},{9,11},{10,... | collective-permute-start | bytes 147464 | tf_op jit(solution)/shard_map/ppermute | solution.py:26
  28.7 3.1 %collective-permute-start = (bf16[8,64,48]{2,1,0:T(8,128)(2,1)S(1)}, bf16[8,64,48]{2,1,0:T(8,128)(2,1)}, u32[]{:S(2)}, u32[]{:S(2)}) collective-permute-start(bf16[8,64,48]{2,1,0:T(8,128)(2,1)S(1)} %get-tuple-element.18), channel_id=1, source_target_pairs={{0,3},{1,0},{2,1},{3,2},{4,7},{5,4},{6,5},{7,6},{8,11},{9,8},{10,9... | collective-permute-start | bytes 147464 | tf_op jit(solution)/shard_map/ppermute | solution.py:26
  31.9 2.6 collective-permute-done
  34.6 1.8 fusion.41
  37.4 13.6 %collective-permute-start.3 = (bf16[8,3072]{1,0:T(8,128)(2,1)S(1)}, bf16[8,3072]{1,0:T(8,128)(2,1)S(1)}, u32[]{:S(2)}, u32[]{:S(2)}) collective-permute-start(bf16[8,3072]{1,0:T(8,128)(2,1)S(1)} %get-tuple-element.38), channel_id=1, source_target_pairs={{0,504},{4,508},{8,0},{12,4},{16,8},{20,12},{24,16},{28,20},{32,24... | collective-permute-start | bytes 147464 | tf_op jit(solution)/shard_map/ppermute | solution.py:49
  51.9 1.9 collective-permute-start.7
  53.8 1.9 collective-permute-start.6
  55.7 5.1 %collective-permute-start.4 = (bf16[8,3072]{1,0:T(8,128)(2,1)S(1)}, bf16[8,3072]{1,0:T(8,128)(2,1)S(1)}, u32[]{:S(2)}, u32[]{:S(2)}) collective-permute-start(bf16[8,3072]{1,0:T(8,128)(2,1)S(1)} %get-tuple-element.37), channel_id=1, source_target_pairs={{0,508},{4,0},{8,4},{12,8},{16,12},{20,16},{24,20},{28,24},{32,28}... | collective-permute-start | bytes 147464 | tf_op jit(solution)/shard_map/ppermute | solution.py:49
  63.9 1.9 collective-permute-start.8
  65.8 12.5 %collective-permute-start.12 = (bf16[8,3072]{1,0:T(8,128)(2,1)S(1)}, bf16[8,3072]{1,0:T(8,128)(2,1)S(1)}, u32[]{:S(2)}, u32[]{:S(2)}) collective-permute-start(bf16[8,3072]{1,0:T(8,128)(2,1)S(1)} %get-tuple-element.29), channel_id=1, source_target_pairs={{0,504},{4,508},{8,0},{12,4},{16,8},{20,12},{24,16},{28,20},{32,24... | collective-permute-start | bytes 147464 | tf_op jit(solution)/shard_map/ppermute | solution.py:49
  78.4 2.5 collective-permute-start.11
  80.9 3.0 %collective-permute-start.9 = (bf16[8,3072]{1,0:T(8,128)(2,1)S(1)}, bf16[8,3072]{1,0:T(8,128)(2,1)S(1)}, u32[]{:S(2)}, u32[]{:S(2)}) collective-permute-start(bf16[8,3072]{1,0:T(8,128)(2,1)S(1)} %get-tuple-element.32), channel_id=1, source_target_pairs={{0,4},{4,8},{8,12},{12,16},{16,20},{20,24},{24,28},{28,32},{32,36}... | collective-permute-start | bytes 147464 | tf_op jit(solution)/shard_map/ppermute | solution.py:49
  87.3 3.7 %all-to-all-start.1 = ((bf16[4,2,12288]{2,1,0:T(2,128)(2,1)}), bf16[4,2,12288]{2,1,0:T(2,128)(2,1)S(1)}, u32[]{:S(2)}, u32[]{:S(2)}) async-start(bf16[4,2,12288]{2,1,0:T(2,128)(2,1)} %reshape.339), calls=%async_computation.1 | async-start | bytes 393216 | tf_op jit(solution)/shard_map/all_to_all | solution.py:196
  92.4 3.7 %all-to-all-done.1 = bf16[4,2,12288]{2,1,0:T(2,128)(2,1)S(1)} async-done(((bf16[4,2,12288]{2,1,0:T(2,128)(2,1)}), bf16[4,2,12288]{2,1,0:T(2,128)(2,1)S(1)}, u32[]{:S(2)}, u32[]{:S(2)}) %all-to-all-start.1) | async-done | bytes 196640 | tf_op jit(solution)/shard_map/all_to_all | solution.py:196
  97.8 3.3 %all-to-all-start.2 = ((f32[4,8,192]{2,1,0:T(8,128)}), f32[4,8,192]{2,1,0:T(8,128)S(1)}, u32[]{:S(2)}, u32[]{:S(2)}) async-start(f32[4,8,192]{2,1,0:T(8,128)} %broadcast_in_dim.83), calls=%async_computation.2 | async-start | bytes 65536 | tf_op jit(solution)/shard_map/all_to_all | solution.py:39
  101.7 3.6 %all-to-all-done.2 = f32[4,8,192]{2,1,0:T(8,128)S(1)} async-done(((f32[4,8,192]{2,1,0:T(8,128)}), f32[4,8,192]{2,1,0:T(8,128)S(1)}, u32[]{:S(2)}, u32[]{:S(2)}) %all-to-all-start.2) | async-done | bytes 24608 | tf_op jit(solution)/shard_map/all_to_all | solution.py:39
  105.7 11.9 %all_to_all.96 = f32[2,64,2,192]{3,1,2,0:T(8,128)S(1)} all-to-all(f32[2,64,2,192]{3,1,2,0:T(8,128)S(1)} %convolution_bitcast_fusion.1), channel_id=1, replica_groups=mesh['sub_0'=8,'sub_1'=8,'sub_2'=2,'grp'=4] {'sub_2'}, dimensions={0} | all-to-all | bytes 393216 | tf_op jit(solution)/shard_map/all_to_all | solution.py:74
  117.8 15.4 %all_to_all.97 = f32[64,2,192]{2,1,0:T(2,128)S(1)} all-to-all(f32[64,2,192]{2,1,0:T(2,128)S(1)} %copy.145), channel_id=1, replica_groups=mesh['sub_0'=8,'sub_1'=8,'sub_2'=2,'grp'=4] {'sub_0','sub_1'}, dimensions={0} | all-to-all | bytes 196608 | tf_op jit(solution)/shard_map/all_to_all | solution.py:82
  134.0 5.6 %all-to-all-start.5 = ((f32[64,2,192]{2,1,0:T(2,128)}), f32[64,2,192]{2,1,0:T(2,128)}, u32[]{:S(2)}, u32[]{:S(2)}) async-start(f32[64,2,192]{2,1,0:T(2,128)} %broadcast_in_dim.84), calls=%async_computation.5 | async-start | bytes 262144 | tf_op jit(solution)/shard_map/all_to_all | solution.py:39
  139.8 11.0 %all-to-all-done.5 = f32[64,2,192]{2,1,0:T(2,128)} async-done(((f32[64,2,192]{2,1,0:T(2,128)}), f32[64,2,192]{2,1,0:T(2,128)}, u32[]{:S(2)}, u32[]{:S(2)}) %all-to-all-start.5) | async-done | bytes 98336 | tf_op jit(solution)/shard_map/all_to_all | solution.py:39
  151.8 6.7 %all_to_all.98 = f32[2,64,2,192]{3,2,1,0:T(2,128)S(1)} all-to-all(f32[2,64,2,192]{3,2,1,0:T(2,128)S(1)} %broadcast_in_dim.85), channel_id=1, replica_groups=mesh['sub_0'=8,'sub_1'=8,'sub_2'=2,'grp'=4] {'sub_2'}, dimensions={0} | all-to-all | bytes 393216 | tf_op jit(solution)/shard_map/all_to_all | solution.py:39
  160.2 14.6 %all_to_all.99 = bf16[4,512,192]{1,2,0:T(8,128)(2,1)S(1)} all-to-all(bf16[4,512,192]{1,2,0:T(8,128)(2,1)S(1)} %broadcast_in_dim.86), channel_id=1, replica_groups=mesh['sub_0'=8,'sub_1'=8,'sub_2'=2,'grp'=4] {'grp'}, dimensions={0} | all-to-all | bytes 1572864 | tf_op jit(solution)/shard_map/all_to_all | solution.py:39
  176.5 2.2 collective-permute-start.15
  178.8 3.7 %collective-permute-start.14 = (bf16[8,64,48]{2,1,0:T(8,128)(2,1)S(1)}, bf16[8,64,48]{2,1,0:T(8,128)(2,1)S(1)}, u32[]{:S(2)}, u32[]{:S(2)}) collective-permute-start(bf16[8,64,48]{2,1,0:T(8,128)(2,1)S(1)} %get-tuple-element.13), channel_id=1, source_target_pairs={{0,2},{1,3},{2,0},{3,1},{4,6},{5,7},{6,4},{7,5},{8,10},{9,11},{10,... | collective-permute-start | bytes 147464 | tf_op jit(solution)/shard_map/ppermute | solution.py:26
  182.4 2.5 collective-permute-start.13
  186.1 3.8 %collective-permute-done.13 = bf16[8,64,48]{2,1,0:T(8,128)(2,1)S(1)} collective-permute-done((bf16[8,64,48]{2,1,0:T(8,128)(2,1)S(1)}, bf16[8,64,48]{2,1,0:T(8,128)(2,1)S(1)}, u32[]{:S(2)}, u32[]{:S(2)}) %collective-permute-start.13) | collective-permute-done | bytes 49184 | tf_op jit(solution)/shard_map/ppermute | solution.py:26
  192.5 2.2 collective-permute-start.16
  194.7 3.1 %collective-permute-start.20 = (bf16[8,3072]{1,0:T(8,128)(2,1)S(1)}, bf16[8,3072]{1,0:T(8,128)(2,1)S(1)}, u32[]{:S(2)}, u32[]{:S(2)}) collective-permute-start(bf16[8,3072]{1,0:T(8,128)(2,1)S(1)} %get-tuple-element.24), channel_id=1, source_target_pairs={{0,8},{4,12},{8,16},{12,20},{16,24},{20,28},{24,32},{28,36},{32,40... | collective-permute-start | bytes 147464 | tf_op jit(solution)/shard_map/ppermute | solution.py:49
  197.8 4.3 %collective-permute-start.19 = (bf16[8,3072]{1,0:T(8,128)(2,1)S(1)}, bf16[8,3072]{1,0:T(8,128)(2,1)S(1)}, u32[]{:S(2)}, u32[]{:S(2)}) collective-permute-start(bf16[8,3072]{1,0:T(8,128)(2,1)S(1)} %get-tuple-element.25), channel_id=1, source_target_pairs={{0,4},{4,8},{8,12},{12,16},{16,20},{20,24},{24,28},{28,32},{32,36}... | collective-permute-start | bytes 147464 | tf_op jit(solution)/shard_map/ppermute | solution.py:49
  202.2 1.9 collective-permute-start.17
  204.1 3.8 %collective-permute-done.17 = bf16[8,3072]{1,0:T(8,128)(2,1)S(1)} collective-permute-done((bf16[8,3072]{1,0:T(8,128)(2,1)S(1)}, bf16[8,3072]{1,0:T(8,128)(2,1)S(1)}, u32[]{:S(2)}, u32[]{:S(2)}) %collective-permute-start.17) | collective-permute-done | bytes 49184 | tf_op jit(solution)/shard_map/ppermute | solution.py:49
  210.7 2.0 collective-permute-start.21
  212.8 9.2 %collective-permute-start.25 = (bf16[8,3072]{1,0:T(8,128)(2,1)S(1)}, bf16[8,3072]{1,0:T(8,128)(2,1)S(1)}, u32[]{:S(2)}, u32[]{:S(2)}) collective-permute-start(bf16[8,3072]{1,0:T(8,128)(2,1)S(1)} %get-tuple-element.19), channel_id=1, source_target_pairs={{0,504},{4,508},{8,0},{12,4},{16,8},{20,12},{24,16},{28,20},{32,24... | collective-permute-start | bytes 147464 | tf_op jit(solution)/shard_map/ppermute | solution.py:49
  222.0 2.5 collective-permute-start.24
  224.5 3.0 %collective-permute-start.22 = (bf16[8,3072]{1,0:T(8,128)(2,1)S(1)}, bf16[8,3072]{1,0:T(8,128)(2,1)S(1)}, u32[]{:S(2)}, u32[]{:S(2)}) collective-permute-start(bf16[8,3072]{1,0:T(8,128)(2,1)S(1)} %get-tuple-element.22), channel_id=1, source_target_pairs={{0,4},{4,8},{8,12},{12,16},{16,20},{20,24},{24,28},{28,32},{32,36}... | collective-permute-start | bytes 147464 | tf_op jit(solution)/shard_map/ppermute | solution.py:49
  230.2 8.3 %all_to_all.100 = bf16[4,2,12288]{2,1,0:T(2,128)(2,1)S(1)} all-to-all(bf16[4,2,12288]{2,1,0:T(2,128)(2,1)S(1)} %reshape.341), channel_id=1, replica_groups=mesh['sub_0'=8,'sub_1'=8,'sub_2'=2,'grp'=4] {'grp'}, dimensions={0} | all-to-all | bytes 393216 | tf_op jit(solution)/shard_map/all_to_all | solution.py:196
  239.5 6.7 %all_to_all.101 = f32[4,8,192]{2,1,0:T(8,128)S(1)} all-to-all(f32[4,8,192]{2,1,0:T(8,128)S(1)} %broadcast_in_dim.87), channel_id=1, replica_groups=mesh['sub_0'=8,'sub_1'=8,'sub_2'=2,'grp'=4] {'grp'}, dimensions={0} | all-to-all | bytes 49152 | tf_op jit(solution)/shard_map/all_to_all | solution.py:39
  246.6 11.9 %all_to_all.102 = f32[2,64,2,192]{3,1,2,0:T(8,128)S(1)} all-to-all(f32[2,64,2,192]{3,1,2,0:T(8,128)S(1)} %convolution_bitcast_fusion), channel_id=1, replica_groups=mesh['sub_0'=8,'sub_1'=8,'sub_2'=2,'grp'=4] {'sub_2'}, dimensions={0} | all-to-all | bytes 393216 | tf_op jit(solution)/shard_map/all_to_all | solution.py:74
  258.6 15.4 %all_to_all.103 = f32[64,2,192]{2,1,0:T(2,128)S(1)} all-to-all(f32[64,2,192]{2,1,0:T(2,128)S(1)} %copy.157), channel_id=1, replica_groups=mesh['sub_0'=8,'sub_1'=8,'sub_2'=2,'grp'=4] {'sub_0','sub_1'}, dimensions={0} | all-to-all | bytes 196608 | tf_op jit(solution)/shard_map/all_to_all | solution.py:82
  274.9 4.6 %all-to-all-start.12 = ((f32[64,2,192]{2,1,0:T(2,128)}), f32[64,2,192]{2,1,0:T(2,128)S(1)}, u32[]{:S(2)}, u32[]{:S(2)}) async-start(f32[64,2,192]{2,1,0:T(2,128)} %broadcast_in_dim.88), calls=%async_computation.12 | async-start | bytes 262144 | tf_op jit(solution)/shard_map/all_to_all | solution.py:39
  279.7 11.4 %all-to-all-done.12 = f32[64,2,192]{2,1,0:T(2,128)S(1)} async-done(((f32[64,2,192]{2,1,0:T(2,128)}), f32[64,2,192]{2,1,0:T(2,128)S(1)}, u32[]{:S(2)}, u32[]{:S(2)}) %all-to-all-start.12) | async-done | bytes 98336 | tf_op jit(solution)/shard_map/all_to_all | solution.py:39
  291.1 6.7 %all_to_all.104 = f32[2,64,2,192]{3,2,1,0:T(2,128)S(1)} all-to-all(f32[2,64,2,192]{3,2,1,0:T(2,128)S(1)} %broadcast_in_dim.89), channel_id=1, replica_groups=mesh['sub_0'=8,'sub_1'=8,'sub_2'=2,'grp'=4] {'sub_2'}, dimensions={0} | all-to-all | bytes 393216 | tf_op jit(solution)/shard_map/all_to_all | solution.py:39
  298.2 1.2 fusion.6
  (193 shorter events, 41.6 us)
Async XLA Ops:
  0.0 19.3 %copy-start = (bf16[1,512,2048]{2,1,0:T(8,128)(2,1)S(1)}, bf16[1,512,2048]{2,1,0:T(8,128)(2,1)}, u32[]{:S(2)}) copy-start(bf16[1,512,2048]{2,1,0:T(8,128)(2,1)} %param.18) | copy-start | bytes 6291460
  0.0 7.6 %copy-start.18 = (s32[128]{0:T(128)S(1)}, s32[128]{0:T(128)}, u32[]{:S(2)}) copy-start(s32[128]{0:T(128)} %param.26) | copy-start | bytes 1540
  0.0 8.1 %copy-start.8 = (s32[128,32,1]{0,2,1:T(1,128)S(1)}, s32[128,32,1]{0,2,1:T(1,128)}, u32[]{:S(2)}) copy-start(s32[128,32,1]{0,2,1:T(1,128)} %param.23) | copy-start | bytes 49156
  0.0 8.2 %copy-start.9 = (s32[128,32]{0,1:T(8,128)S(1)}, s32[128,32]{0,1:T(8,128)}, u32[]{:S(2)}) copy-start(s32[128,32]{0,1:T(8,128)} %param.24) | copy-start | bytes 49156
  2.2 17.1 %all-to-all-start = ((bf16[4,512,192]{1,2,0:T(8,128)(2,1)}), bf16[4,512,192]{1,2,0:T(8,128)(2,1)S(1)}, u32[]{:S(2)}, u32[]{:S(2)}) async-start(bf16[4,512,192]{1,2,0:T(8,128)(2,1)} %broadcast_in_dim.48), calls=%async_computation | async-start | bytes 1572864 | tf_op jit(solution)/shard_map/all_to_all | solution.py:39
  7.0 12.4 %copy-start.3 = (f32[1,512,192]{1,2,0:T(8,128)S(1)}, f32[1,512,192]{1,2,0:T(8,128)}, u32[]{:S(2)}) copy-start(f32[1,512,192]{1,2,0:T(8,128)} %param.19) | copy-start | bytes 1179652
  19.2 44.4 %copy-start.6 = (bf16[5,8,16]{2,1,0:T(8,128)(2,1)}, bf16[5,8,16]{2,1,0:T(8,128)(2,1)S(1)}, u32[]{:S(2)}) copy-start(bf16[5,8,16]{2,1,0:T(8,128)(2,1)S(1)} %convolution_convert_fusion.8) | copy-start | bytes 3844
  21.1 10.8 %collective-permute-start.2 = (bf16[8,64,48]{2,1,0:T(8,128)(2,1)S(1)}, bf16[8,64,48]{2,1,0:T(8,128)(2,1)S(1)}, u32[]{:S(2)}, u32[]{:S(2)}) collective-permute-start(bf16[8,64,48]{2,1,0:T(8,128)(2,1)S(1)} %get-tuple-element.16), channel_id=1, source_target_pairs={{0,1},{1,2},{2,3},{3,0},{4,5},{5,6},{6,7},{7,4},{8,9},{9,10},{10,1... | collective-permute-start | bytes 147464 | tf_op jit(solution)/shard_map/ppermute | solution.py:26
  24.4 7.5 %collective-permute-start.1 = (bf16[8,64,48]{2,1,0:T(8,128)(2,1)S(1)}, bf16[8,64,48]{2,1,0:T(8,128)(2,1)S(1)}, u32[]{:S(2)}, u32[]{:S(2)}) collective-permute-start(bf16[8,64,48]{2,1,0:T(8,128)(2,1)S(1)} %get-tuple-element.17), channel_id=1, source_target_pairs={{0,2},{1,3},{2,0},{3,1},{4,6},{5,7},{6,4},{7,5},{8,10},{9,11},{10,... | collective-permute-start | bytes 147464 | tf_op jit(solution)/shard_map/ppermute | solution.py:26
  28.7 5.8 %collective-permute-start = (bf16[8,64,48]{2,1,0:T(8,128)(2,1)S(1)}, bf16[8,64,48]{2,1,0:T(8,128)(2,1)}, u32[]{:S(2)}, u32[]{:S(2)}) collective-permute-start(bf16[8,64,48]{2,1,0:T(8,128)(2,1)S(1)} %get-tuple-element.18), channel_id=1, source_target_pairs={{0,3},{1,0},{2,1},{3,2},{4,7},{5,4},{6,5},{7,6},{8,11},{9,8},{10,9... | collective-permute-start | bytes 147464 | tf_op jit(solution)/shard_map/ppermute | solution.py:26
  31.9 53.3 %copy-start.10 = (s32[32]{0:T(128)}, s32[32]{0:T(128)S(1)}, u32[]{:S(2)}) copy-start(s32[32]{0:T(128)S(1)} %fusion.82) | copy-start | bytes 388
  36.4 26.4 %copy-start.12 = (f32[16,64]{1,0:T(8,128)S(1)}, f32[16,64]{1,0:T(8,128)}, u32[]{:S(2)}) copy-start(f32[16,64]{1,0:T(8,128)} %and_convert_fusion) | copy-start | bytes 12292
  37.4 23.4 %collective-permute-start.3 = (bf16[8,3072]{1,0:T(8,128)(2,1)S(1)}, bf16[8,3072]{1,0:T(8,128)(2,1)S(1)}, u32[]{:S(2)}, u32[]{:S(2)}) collective-permute-start(bf16[8,3072]{1,0:T(8,128)(2,1)S(1)} %get-tuple-element.38), channel_id=1, source_target_pairs={{0,504},{4,508},{8,0},{12,4},{16,8},{20,12},{24,16},{28,20},{32,24... | collective-permute-start | bytes 147464 | tf_op jit(solution)/shard_map/ppermute | solution.py:49
  51.9 11.5 %copy-start.19 = (f32[16]{0:T(128)}, f32[16]{0:T(128)S(1)}, u32[]{:S(2)}) copy-start(f32[16]{0:T(128)S(1)} %fusion.30) | copy-start | bytes 196
  51.9 9.9 %collective-permute-start.7 = (bf16[8,3072]{1,0:T(8,128)(2,1)S(1)}, bf16[8,3072]{1,0:T(8,128)(2,1)S(1)}, u32[]{:S(2)}, u32[]{:S(2)}) collective-permute-start(bf16[8,3072]{1,0:T(8,128)(2,1)S(1)} %get-tuple-element.34), channel_id=1, source_target_pairs={{0,8},{4,12},{8,16},{12,20},{16,24},{20,28},{24,32},{28,36},{32,40... | collective-permute-start | bytes 147464 | tf_op jit(solution)/shard_map/ppermute | solution.py:49
  53.8 8.0 %collective-permute-start.6 = (bf16[8,3072]{1,0:T(8,128)(2,1)S(1)}, bf16[8,3072]{1,0:T(8,128)(2,1)S(1)}, u32[]{:S(2)}, u32[]{:S(2)}) collective-permute-start(bf16[8,3072]{1,0:T(8,128)(2,1)S(1)} %get-tuple-element.35), channel_id=1, source_target_pairs={{0,4},{4,8},{8,12},{12,16},{16,20},{20,24},{24,28},{28,32},{32,36}... | collective-permute-start | bytes 147464 | tf_op jit(solution)/shard_map/ppermute | solution.py:49
  55.7 6.0 %collective-permute-start.5 = (bf16[8,3072]{1,0:T(8,128)(2,1)S(1)}, bf16[8,3072]{1,0:T(8,128)(2,1)S(1)}, u32[]{:S(2)}, u32[]{:S(2)}) collective-permute-start(bf16[8,3072]{1,0:T(8,128)(2,1)S(1)} %get-tuple-element.36), channel_id=1, source_target_pairs={{0,0},{4,4},{8,8},{12,12},{16,16},{20,20},{24,24},{28,28},{32,32},... | collective-permute-start | bytes 147464 | tf_op jit(solution)/shard_map/ppermute | solution.py:49
  55.7 6.0 %collective-permute-start.4 = (bf16[8,3072]{1,0:T(8,128)(2,1)S(1)}, bf16[8,3072]{1,0:T(8,128)(2,1)S(1)}, u32[]{:S(2)}, u32[]{:S(2)}) collective-permute-start(bf16[8,3072]{1,0:T(8,128)(2,1)S(1)} %get-tuple-element.37), channel_id=1, source_target_pairs={{0,508},{4,0},{8,4},{12,8},{16,12},{20,16},{24,20},{28,24},{32,28}... | collective-permute-start | bytes 147464 | tf_op jit(solution)/shard_map/ppermute | solution.py:49
  63.9 27.1 %copy-start.17 = (pred[128]{0:T(512)(128)(4,1)S(1)}, pred[128]{0:T(512)(128)(4,1)}, u32[]{:S(2)}) copy-start(pred[128]{0:T(512)(128)(4,1)} %copy-done.16) | copy-start | bytes 388
  63.9 27.7 %copy-start.14 = (s32[128,8]{0,1:T(8,128)S(1)}, s32[128,8]{0,1:T(8,128)}, u32[]{:S(2)}) copy-start(s32[128,8]{0,1:T(8,128)} %param.27) | copy-start | bytes 12292
  63.9 20.1 %collective-permute-start.8 = (bf16[8,3072]{1,0:T(8,128)(2,1)S(1)}, bf16[8,3072]{1,0:T(8,128)(2,1)S(1)}, u32[]{:S(2)}, u32[]{:S(2)}) collective-permute-start(bf16[8,3072]{1,0:T(8,128)(2,1)S(1)} %get-tuple-element.33), channel_id=1, source_target_pairs={{0,8},{4,12},{8,16},{12,20},{16,24},{20,28},{24,32},{28,36},{32,40... | collective-permute-start | bytes 147464 | tf_op jit(solution)/shard_map/ppermute | solution.py:49
  65.8 19.3 %collective-permute-start.12 = (bf16[8,3072]{1,0:T(8,128)(2,1)S(1)}, bf16[8,3072]{1,0:T(8,128)(2,1)S(1)}, u32[]{:S(2)}, u32[]{:S(2)}) collective-permute-start(bf16[8,3072]{1,0:T(8,128)(2,1)S(1)} %get-tuple-element.29), channel_id=1, source_target_pairs={{0,504},{4,508},{8,0},{12,4},{16,8},{20,12},{24,16},{28,20},{32,24... | collective-permute-start | bytes 147464 | tf_op jit(solution)/shard_map/ppermute | solution.py:49
  78.4 6.8 %collective-permute-start.11 = (bf16[8,3072]{1,0:T(8,128)(2,1)S(1)}, bf16[8,3072]{1,0:T(8,128)(2,1)S(1)}, u32[]{:S(2)}, u32[]{:S(2)}) collective-permute-start(bf16[8,3072]{1,0:T(8,128)(2,1)S(1)} %get-tuple-element.30), channel_id=1, source_target_pairs={{0,508},{4,0},{8,4},{12,8},{16,12},{20,16},{24,20},{28,24},{32,28}... | collective-permute-start | bytes 147464 | tf_op jit(solution)/shard_map/ppermute | solution.py:49
  80.9 4.2 %collective-permute-start.10 = (bf16[8,3072]{1,0:T(8,128)(2,1)S(1)}, bf16[8,3072]{1,0:T(8,128)(2,1)S(1)}, u32[]{:S(2)}, u32[]{:S(2)}) collective-permute-start(bf16[8,3072]{1,0:T(8,128)(2,1)S(1)} %get-tuple-element.31), channel_id=1, source_target_pairs={{0,0},{4,4},{8,8},{12,12},{16,16},{20,20},{24,24},{28,28},{32,32},... | collective-permute-start | bytes 147464 | tf_op jit(solution)/shard_map/ppermute | solution.py:49
  80.9 4.2 %collective-permute-start.9 = (bf16[8,3072]{1,0:T(8,128)(2,1)S(1)}, bf16[8,3072]{1,0:T(8,128)(2,1)S(1)}, u32[]{:S(2)}, u32[]{:S(2)}) collective-permute-start(bf16[8,3072]{1,0:T(8,128)(2,1)S(1)} %get-tuple-element.32), channel_id=1, source_target_pairs={{0,4},{4,8},{8,12},{12,16},{16,20},{20,24},{24,28},{28,32},{32,36}... | collective-permute-start | bytes 147464 | tf_op jit(solution)/shard_map/ppermute | solution.py:49
  86.3 10.6 %copy-start.5 = (bf16[1,8,512]{2,1,0:T(8,128)(2,1)S(1)}, bf16[1,8,512]{2,1,0:T(8,128)(2,1)}, u32[]{:S(2)}) copy-start(bf16[1,8,512]{2,1,0:T(8,128)(2,1)} %param.22) | copy-start | bytes 24580
  87.3 8.8 %all-to-all-start.1 = ((bf16[4,2,12288]{2,1,0:T(2,128)(2,1)}), bf16[4,2,12288]{2,1,0:T(2,128)(2,1)S(1)}, u32[]{:S(2)}, u32[]{:S(2)}) async-start(bf16[4,2,12288]{2,1,0:T(2,128)(2,1)} %reshape.339), calls=%async_computation.1 | async-start | bytes 393216 | tf_op jit(solution)/shard_map/all_to_all | solution.py:196
  97.8 7.5 %all-to-all-start.2 = ((f32[4,8,192]{2,1,0:T(8,128)}), f32[4,8,192]{2,1,0:T(8,128)S(1)}, u32[]{:S(2)}, u32[]{:S(2)}) async-start(f32[4,8,192]{2,1,0:T(8,128)} %broadcast_in_dim.83), calls=%async_computation.2 | async-start | bytes 65536 | tf_op jit(solution)/shard_map/all_to_all | solution.py:39
  117.6 41.3 %copy-start.1 = (f32[1,512,192]{1,2,0:T(8,128)S(1)}, f32[1,512,192]{1,2,0:T(8,128)}, u32[]{:S(2)}) copy-start(f32[1,512,192]{1,2,0:T(8,128)} %param.20) | copy-start | bytes 1179652
  134.0 16.9 %all-to-all-start.5 = ((f32[64,2,192]{2,1,0:T(2,128)}), f32[64,2,192]{2,1,0:T(2,128)}, u32[]{:S(2)}, u32[]{:S(2)}) async-start(f32[64,2,192]{2,1,0:T(2,128)} %broadcast_in_dim.84), calls=%async_computation.5 | async-start | bytes 262144 | tf_op jit(solution)/shard_map/all_to_all | solution.py:39
  160.1 14.7 %copy-start.4 = (f32[1,512,192]{1,2,0:T(8,128)S(1)}, f32[1,512,192]{1,2,0:T(8,128)}, u32[]{:S(2)}) copy-start(f32[1,512,192]{1,2,0:T(8,128)} %param.19) | copy-start | bytes 1179652
  176.5 8.4 %collective-permute-start.15 = (bf16[8,64,48]{2,1,0:T(8,128)(2,1)S(1)}, bf16[8,64,48]{2,1,0:T(8,128)(2,1)S(1)}, u32[]{:S(2)}, u32[]{:S(2)}) collective-permute-start(bf16[8,64,48]{2,1,0:T(8,128)(2,1)S(1)} %get-tuple-element.12), channel_id=1, source_target_pairs={{0,1},{1,2},{2,3},{3,0},{4,5},{5,6},{6,7},{7,4},{8,9},{9,10},{10,1... | collective-permute-start | bytes 147464 | tf_op jit(solution)/shard_map/ppermute | solution.py:26
  178.8 7.3 %collective-permute-start.14 = (bf16[8,64,48]{2,1,0:T(8,128)(2,1)S(1)}, bf16[8,64,48]{2,1,0:T(8,128)(2,1)S(1)}, u32[]{:S(2)}, u32[]{:S(2)}) collective-permute-start(bf16[8,64,48]{2,1,0:T(8,128)(2,1)S(1)} %get-tuple-element.13), channel_id=1, source_target_pairs={{0,2},{1,3},{2,0},{3,1},{4,6},{5,7},{6,4},{7,5},{8,10},{9,11},{10,... | collective-permute-start | bytes 147464 | tf_op jit(solution)/shard_map/ppermute | solution.py:26
  182.4 7.4 %collective-permute-start.13 = (bf16[8,64,48]{2,1,0:T(8,128)(2,1)S(1)}, bf16[8,64,48]{2,1,0:T(8,128)(2,1)S(1)}, u32[]{:S(2)}, u32[]{:S(2)}) collective-permute-start(bf16[8,64,48]{2,1,0:T(8,128)(2,1)S(1)} %get-tuple-element.14), channel_id=1, source_target_pairs={{0,3},{1,0},{2,1},{3,2},{4,7},{5,4},{6,5},{7,6},{8,11},{9,8},{10,9... | collective-permute-start | bytes 147464 | tf_op jit(solution)/shard_map/ppermute | solution.py:26
  190.8 18.1 %copy-start.7 = (bf16[5,8,16]{2,1,0:T(8,128)(2,1)S(1)}, bf16[5,8,16]{2,1,0:T(8,128)(2,1)}, u32[]{:S(2)}) copy-start(bf16[5,8,16]{2,1,0:T(8,128)(2,1)} %copy-done.6) | copy-start | bytes 3844
  192.5 11.6 %collective-permute-start.16 = (bf16[8,3072]{1,0:T(8,128)(2,1)S(1)}, bf16[8,3072]{1,0:T(8,128)(2,1)S(1)}, u32[]{:S(2)}, u32[]{:S(2)}) collective-permute-start(bf16[8,3072]{1,0:T(8,128)(2,1)S(1)} %get-tuple-element.28), channel_id=1, source_target_pairs={{0,504},{4,508},{8,0},{12,4},{16,8},{20,12},{24,16},{28,20},{32,24... | collective-permute-start | bytes 147464 | tf_op jit(solution)/shard_map/ppermute | solution.py:49
  194.7 13.2 %collective-permute-start.20 = (bf16[8,3072]{1,0:T(8,128)(2,1)S(1)}, bf16[8,3072]{1,0:T(8,128)(2,1)S(1)}, u32[]{:S(2)}, u32[]{:S(2)}) collective-permute-start(bf16[8,3072]{1,0:T(8,128)(2,1)S(1)} %get-tuple-element.24), channel_id=1, source_target_pairs={{0,8},{4,12},{8,16},{12,20},{16,24},{20,28},{24,32},{28,36},{32,40... | collective-permute-start | bytes 147464 | tf_op jit(solution)/shard_map/ppermute | solution.py:49
  197.8 10.1 %collective-permute-start.19 = (bf16[8,3072]{1,0:T(8,128)(2,1)S(1)}, bf16[8,3072]{1,0:T(8,128)(2,1)S(1)}, u32[]{:S(2)}, u32[]{:S(2)}) collective-permute-start(bf16[8,3072]{1,0:T(8,128)(2,1)S(1)} %get-tuple-element.25), channel_id=1, source_target_pairs={{0,4},{4,8},{8,12},{12,16},{16,20},{20,24},{24,28},{28,32},{32,36}... | collective-permute-start | bytes 147464 | tf_op jit(solution)/shard_map/ppermute | solution.py:49
  202.1 5.7 %collective-permute-start.18 = (bf16[8,3072]{1,0:T(8,128)(2,1)S(1)}, bf16[8,3072]{1,0:T(8,128)(2,1)S(1)}, u32[]{:S(2)}, u32[]{:S(2)}) collective-permute-start(bf16[8,3072]{1,0:T(8,128)(2,1)S(1)} %get-tuple-element.26), channel_id=1, source_target_pairs={{0,0},{4,4},{8,8},{12,12},{16,16},{20,20},{24,24},{28,28},{32,32},... | collective-permute-start | bytes 147464 | tf_op jit(solution)/shard_map/ppermute | solution.py:49
  202.2 5.7 %collective-permute-start.17 = (bf16[8,3072]{1,0:T(8,128)(2,1)S(1)}, bf16[8,3072]{1,0:T(8,128)(2,1)S(1)}, u32[]{:S(2)}, u32[]{:S(2)}) collective-permute-start(bf16[8,3072]{1,0:T(8,128)(2,1)S(1)} %get-tuple-element.27), channel_id=1, source_target_pairs={{0,508},{4,0},{8,4},{12,8},{16,12},{20,16},{24,20},{28,24},{32,28}... | collective-permute-start | bytes 147464 | tf_op jit(solution)/shard_map/ppermute | solution.py:49
  209.0 19.8 %copy-start.11 = (s32[32]{0:T(128)S(1)}, s32[32]{0:T(128)}, u32[]{:S(2)}) copy-start(s32[32]{0:T(128)} %copy-done.10) | copy-start | bytes 388
  210.7 16.8 %collective-permute-start.21 = (bf16[8,3072]{1,0:T(8,128)(2,1)S(1)}, bf16[8,3072]{1,0:T(8,128)(2,1)S(1)}, u32[]{:S(2)}, u32[]{:S(2)}) collective-permute-start(bf16[8,3072]{1,0:T(8,128)(2,1)S(1)} %get-tuple-element.23), channel_id=1, source_target_pairs={{0,8},{4,12},{8,16},{12,20},{16,24},{20,28},{24,32},{28,36},{32,40... | collective-permute-start | bytes 147464 | tf_op jit(solution)/shard_map/ppermute | solution.py:49
  212.8 16.0 %collective-permute-start.25 = (bf16[8,3072]{1,0:T(8,128)(2,1)S(1)}, bf16[8,3072]{1,0:T(8,128)(2,1)S(1)}, u32[]{:S(2)}, u32[]{:S(2)}) collective-permute-start(bf16[8,3072]{1,0:T(8,128)(2,1)S(1)} %get-tuple-element.19), channel_id=1, source_target_pairs={{0,504},{4,508},{8,0},{12,4},{16,8},{20,12},{24,16},{28,20},{32,24... | collective-permute-start | bytes 147464 | tf_op jit(solution)/shard_map/ppermute | solution.py:49
  222.0 6.8 %collective-permute-start.24 = (bf16[8,3072]{1,0:T(8,128)(2,1)S(1)}, bf16[8,3072]{1,0:T(8,128)(2,1)S(1)}, u32[]{:S(2)}, u32[]{:S(2)}) collective-permute-start(bf16[8,3072]{1,0:T(8,128)(2,1)S(1)} %get-tuple-element.20), channel_id=1, source_target_pairs={{0,508},{4,0},{8,4},{12,8},{16,12},{20,16},{24,20},{28,24},{32,28}... | collective-permute-start | bytes 147464 | tf_op jit(solution)/shard_map/ppermute | solution.py:49
  224.5 4.2 %collective-permute-start.23 = (bf16[8,3072]{1,0:T(8,128)(2,1)S(1)}, bf16[8,3072]{1,0:T(8,128)(2,1)S(1)}, u32[]{:S(2)}, u32[]{:S(2)}) collective-permute-start(bf16[8,3072]{1,0:T(8,128)(2,1)S(1)} %get-tuple-element.21), channel_id=1, source_target_pairs={{0,0},{4,4},{8,8},{12,12},{16,16},{20,20},{24,24},{28,28},{32,32},... | collective-permute-start | bytes 147464 | tf_op jit(solution)/shard_map/ppermute | solution.py:49
  224.5 4.2 %collective-permute-start.22 = (bf16[8,3072]{1,0:T(8,128)(2,1)S(1)}, bf16[8,3072]{1,0:T(8,128)(2,1)S(1)}, u32[]{:S(2)}, u32[]{:S(2)}) collective-permute-start(bf16[8,3072]{1,0:T(8,128)(2,1)S(1)} %get-tuple-element.22), channel_id=1, source_target_pairs={{0,4},{4,8},{8,12},{12,16},{16,20},{20,24},{24,28},{28,32},{32,36}... | collective-permute-start | bytes 147464 | tf_op jit(solution)/shard_map/ppermute | solution.py:49
  258.5 39.7 %copy-start.2 = (f32[512,192]{0,1:T(8,128)S(1)}, f32[512,192]{0,1:T(8,128)}, u32[]{:S(2)}) copy-start(f32[512,192]{0,1:T(8,128)} %get-tuple-element.44) | copy-start | bytes 1179652
  274.9 16.2 %all-to-all-start.12 = ((f32[64,2,192]{2,1,0:T(2,128)}), f32[64,2,192]{2,1,0:T(2,128)S(1)}, u32[]{:S(2)}, u32[]{:S(2)}) async-start(f32[64,2,192]{2,1,0:T(2,128)} %broadcast_in_dim.88), calls=%async_computation.12 | async-start | bytes 262144 | tf_op jit(solution)/shard_map/all_to_all | solution.py:39
  (3 other events, 6.1 us)
